TPU v7x, 32 devices: a whole 2x2x4 slice. The times are simulated.
32 devices in a mesh: member: 2 (over x), wave: 16 (over z, y, core).
Axes of the slice: x: 2, y: 2, z: 4, core: 2. Of those that a mesh axis runs over, the one named last changes fastest.
Arguments:
- vorticity: bfloat16 [2560, 32, 1280], P(('member', 'wave')), parts along dimension 0, may hold values from -6 to 6
- divergence: bfloat16 [2560, 32, 1280], P(('member', 'wave')), parts along dimension 0, may hold values from -6 to 6
- legendre: bfloat16 [1280, 16, 1280], P('wave'), may hold values from -0.0068359375 to 0.0068359375
- wave_of_slot: int32 [1280], replicated, may hold values from 0 to 1279, as said below
- cycle_points: int32 [16], P('wave'), may hold values from 20 to 5136, as said below
- cos_squared: float32 [16], P('wave'), may hold values from 0.25 to 1
Outputs:
- grid: bfloat16 [32, 96, 5136], P(('member', 'wave')), parts along dimension 0
There are 2 independent parts, one for each index of `member`. A program takes and returns all parts, laid end to end along the dimension named above; an argument that names none is the same for every part. Nothing has to cross between parts.
Inputs may be any that keep to these rules, and one draw needn't show every extreme that they name: `wave_of_slot`: each wavenumber appears in exactly one slot. `cycle_points`: every count is a multiple of 4; some cycle has 5136 points.
All inputs are finite; a program needn't handle non-finite values.
Results may differ from a plain program's by a relative error of at most 0.0063.
Values may be sent and summed in bfloat16 or wider, within the bound.
A program may use at most 192 MiB of HBM per device.

v0:
```python
import jax
import jax.numpy as jnp
from jax import lax
from jax.sharding import PartitionSpec as P

NWAVE = 1280
NLON = 5136


def spectral_fields(zeta_in, delta_in, waves):
    columns = zeta_in.shape[-1]
    levels = zeta_in.shape[1] // 2
    degree = waves[:, None] + jnp.arange(columns, dtype=jnp.int32)[None, :]
    living = degree < NWAVE
    positive = living & (degree > 0)
    wave_f = waves.astype(jnp.float32)[:, None]
    degree_f = degree.astype(jnp.float32)
    radius = NWAVE / 4.0
    inverse = jnp.where(positive, -radius / jnp.maximum(degree_f * (degree_f + 1.0), 1.0), 0.0)
    quotient = jnp.maximum(degree_f * degree_f - wave_f * wave_f, 0.0) / jnp.maximum(
        4.0 * degree_f * degree_f - 1.0, 1.0
    )
    coupling = jnp.where(positive, jnp.sqrt(quotient), 0.0)
    coupling_next = jnp.concatenate([coupling[:, 1:], jnp.zeros_like(coupling[:, :1])], axis=1)
    upper_coef = ((degree_f + 2.0) * coupling_next)[:, None, :]
    lower_coef = ((degree_f - 1.0) * coupling)[:, None, :]
    live_mask = living.astype(jnp.float32)[:, None, :]
    zeta = zeta_in.astype(jnp.float32) * live_mask
    delta = delta_in.astype(jnp.float32) * live_mask
    stream = zeta * inverse[:, None, :]
    potential = delta * inverse[:, None, :]

    def meridional(values):
        shifted_up = jnp.concatenate([values[..., 1:], jnp.zeros_like(values[..., :1])], axis=-1)
        shifted_down = jnp.concatenate([jnp.zeros_like(values[..., :1]), values[..., :-1]], axis=-1)
        return (upper_coef * shifted_up - lower_coef * shifted_down) * live_mask

    stream_h = meridional(stream)
    potential_h = meridional(potential)
    wave_three = waves.astype(jnp.float32)[:, None, None]
    u_real = -wave_three * potential[:, levels:] - stream_h[:, :levels]
    u_imag = wave_three * potential[:, :levels] - stream_h[:, levels:]
    v_real = -wave_three * stream[:, levels:] + potential_h[:, :levels]
    v_imag = wave_three * stream[:, :levels] + potential_h[:, levels:]
    return jnp.concatenate([u_real, u_imag, v_real, v_imag, zeta, delta], axis=1).astype(
        jnp.bfloat16
    )


def derive(fourier, waves, cosine_sq):
    cycles, slots, columns = fourier.shape
    levels = columns // 8
    groups = fourier.reshape(cycles, slots, 4, 2, levels)
    wind_u = groups[:, :, 0]
    wind_v = groups[:, :, 1]
    zeta_f = groups[:, :, 2]
    delta_f = groups[:, :, 3]
    scale = (waves.astype(jnp.float32) / (NWAVE / 4.0))[None, :, None]
    u_lon = jnp.stack([-scale * wind_u[:, :, 1], scale * wind_u[:, :, 0]], axis=2)
    v_lon = jnp.stack([-scale * wind_v[:, :, 1], scale * wind_v[:, :, 0]], axis=2)
    factor = cosine_sq[:, None, None, None]
    u_lat = v_lon / factor - zeta_f
    v_lat = delta_f - u_lon / factor
    stacked = jnp.stack([wind_u, wind_v, u_lon, v_lon, u_lat, v_lat], axis=2)
    return stacked.reshape(cycles, slots, 12 * levels)


def cycle_basis(waves, points):
    positions = jnp.arange(NLON, dtype=jnp.int32)
    phase = waves[:, None] * positions[None, :] % points
    theta = 2.0 * jnp.pi / points.astype(jnp.float32) * phase.astype(jnp.float32)
    keeping = (2 * waves[:, None] < points) & (positions[None, :] < points)
    weight = jnp.where(waves == 0, 1.0, 2.0)[:, None]
    cosine = jnp.where(keeping, weight * jnp.cos(theta), 0.0)
    sine = jnp.where(keeping, -weight * jnp.sin(theta), 0.0)
    return jnp.stack([cosine, sine]).astype(jnp.bfloat16)


def synthesize(fields, waves, points, pieces):
    slot_count = fields.shape[1]
    levels = fields.shape[2] // 12
    span = slot_count // pieces

    def one_cycle(item):
        cycle_fields, count = item
        packed = cycle_fields.astype(jnp.bfloat16).reshape(slot_count, 6, 2, levels)

        def add_segment(index, summed):
            start = index * span
            segment = lax.dynamic_slice_in_dim(packed, start, span, 0)
            segment_waves = lax.dynamic_slice_in_dim(waves, start, span, 0)
            basis = cycle_basis(segment_waves, count)
            return summed + jnp.einsum(
                "sfrl,rsp->flp", segment, basis, preferred_element_type=jnp.float32
            )

        summed = lax.fori_loop(0, pieces, add_segment, jnp.zeros((6, levels, NLON), jnp.float32))
        return summed.reshape(6 * levels, NLON)

    return lax.map(one_cycle, (fields, points))


def body(vorticity, divergence, legendre, wave_of_slot, cycle_points, cos_squared):
    slot_count = vorticity.shape[0]
    offset = lax.axis_index("wave") * slot_count
    own_waves = lax.dynamic_slice_in_dim(wave_of_slot, offset, slot_count, 0)
    spec = spectral_fields(vorticity, divergence, own_waves)
    fourier = jnp.einsum("sck,slk->lsc", spec, legendre, preferred_element_type=jnp.float32)
    arrived = lax.all_to_all(fourier, "wave", split_axis=0, concat_axis=1, tiled=True)
    fields = derive(arrived, wave_of_slot, cos_squared)
    summed = synthesize(fields, wave_of_slot, cycle_points, 4)
    return summed.astype(jnp.bfloat16)


def solution(mesh):
    return jax.shard_map(
        body,
        mesh=mesh,
        in_specs=(
            P(("member", "wave"), None, None),
            P(("member", "wave"), None, None),
            P("wave", None, None),
            P(),
            P("wave"),
            P("wave"),
        ),
        out_specs=P(("member", "wave"), None, None),
        check_vma=False,
    )
```

profile of v0, /device:TPU:0, one launch (start us, length us, event | category | flops | bytes accessed | tf_op | source)
XLA Modules:
  0.0 571.8 jit_solution(153109308669183150)
XLA Ops:
  1.1 1.2 fusion.36
  2.4 1.0 pad_multiply_fusion
  3.4 13.8 %fusion.18 = (f32[80,32,1280]{2,1,0:T(8,128)}, f32[80,32,1280]{2,1,0:T(8,128)}) fusion(bf16[80,32,1280]{2,1,0:T(8,128)(2,1)} %param.9, f32[80,1280]{1,0:T(8,128)S(1)} %get-tuple-element.254, f32[80,1280]{1,0:T(8,128)S(1)} %fusion.40, bf16[80,32,1280]{2,1,0:T(8,128)(2,1)} %param.8), kind=kLoop, calls=%fused_computation.31 | loop fusion | flops 19660800 | bytes 40140800 | tf_op jit(solution)/shard_map/mul | solution.py:31
  17.2 36.5 %fusion.58 = (f32[80,32,1279]{2,1,0:T(8,128)}, f32[80,32,1279]{2,1,0:T(8,128)}, f32[80,32,1279]{2,1,0:T(8,128)}, f32[80,32,1279]{2,1,0:T(8,128)}) fusion(f32[80,32,1280]{2,1,0:T(8,128)} %get-tuple-element.227, f32[80,32,1280]{2,1,0:T(8,128)} %get-tuple-element.228), kind=kLoop, calls=%fused_computation.101 | loop fusion | bytes 104775680 | tf_op jit(solution)/shard_map/slice | solution.py:34
  53.7 27.6 %subtract_multiply_fusion = (f32[80,32,1280]{2,1,0:T(8,128)}, f32[80,32,1280]{2,1,0:T(8,128)}) fusion(f32[80,32,1279]{2,1,0:T(8,128)} %get-tuple-element.222, f32[80,32,1279]{2,1,0:T(8,128)} %get-tuple-element.221, f32[80,1280]{1,0:T(8,128)} %get-tuple-element.250, f32[80,1280]{1,0:T(8,128)} %get-tuple-element.253, f32[80,1280]{1,0:T(8,128)} %copy-done.2, ...), kind=kLoop, calls=%fused_computation.24 | loop fusion | flops 26214400 | bytes 79831040 | tf_op jit(solution)/shard_map/mul | solution.py:36
  81.3 7.1 %fusion.25 = bf16[80,128,1280]{2,1,0:T(8,128)(2,1)} fusion(f32[80,32,1280]{2,1,0:T(8,128)} %get-tuple-element.226, f32[80,32,1280]{2,1,0:T(8,128)} %get-tuple-element.227, f32[80]{0:T(128)S(1)} %get-tuple-element.251), kind=kLoop, calls=%fused_computation.46 | loop fusion | flops 4915199 | bytes 16384320
  88.5 7.8 %fusion.26 = bf16[80,128,1280]{2,1,0:T(8,128)(2,1)} fusion(bf16[80,128,1280]{2,1,0:T(8,128)(2,1)} %fusion.25, f32[80,32,1280]{2,1,0:T(8,128)} %get-tuple-element.226, f32[80,32,1280]{2,1,0:T(8,128)} %get-tuple-element.227, f32[80]{0:T(128)S(1)} %get-tuple-element.217), kind=kLoop, calls=%fused_computation.47 | loop fusion | flops 4915200 | bytes 16384320
  97.2 1.3 slice-done.1
  98.5 1.2 slice-done.2
  99.7 2.1 fusion.27
  101.8 2.2 fusion.28
  104.0 1.3 slice-done.5
  105.3 4.9 fusion.20
  110.2 7.8 %fusion.19 = bf16[80,128,1280]{2,1,0:T(8,128)(2,1)} fusion(bf16[80,128,1280]{2,1,0:T(8,128)(2,1)} %fusion.20, bf16[80,32,1280]{2,1,0:T(8,128)(2,1)} %param.9, f32[80,1280]{1,0:T(8,128)S(1)} %copy-done.3), kind=kLoop, calls=%fused_computation.32 | loop fusion | flops 9830400 | bytes 13516800 | tf_op jit(solution)/shard_map/concatenate | solution.py:45
  118.0 14.0 %convolution_bitcast_fusion.1 = f32[16,80,128]{2,0,1:T(8,128)} fusion(bf16[80,128,1280]{2,1,0:T(8,128)(2,1)} %fusion.19, bf16[80,16,1280]{2,1,0:T(8,128)(2,1)S(1)} %copy-done), kind=kOutput, calls=%fused_computation.50 | convolution fusion | flops 419430400 | bytes 30146560 | tf_op jit(solution)/shard_map/sck,slk->lsc/dot_general | solution.py:108
  132.0 2.1 copy.8
  134.1 7.4 %all-to-all-start = ((f32[16,80,128]{2,1,0:T(8,128)}), f32[16,80,128]{2,1,0:T(8,128)}, u32[]{:S(2)}, u32[]{:S(2)}) async-start(f32[16,80,128]{2,1,0:T(8,128)} %copy.8), calls=%async_computation | async-start | bytes 1310720 | tf_op jit(solution)/shard_map/all_to_all | solution.py:109
  143.0 15.3 %all-to-all-done = f32[16,80,128]{2,1,0:T(8,128)} async-done(((f32[16,80,128]{2,1,0:T(8,128)}), f32[16,80,128]{2,1,0:T(8,128)}, u32[]{:S(2)}, u32[]{:S(2)}) %all-to-all-start) | async-done | bytes 655392 | tf_op jit(solution)/shard_map/all_to_all | solution.py:109
  158.2 2.5 copy.9
  160.7 2.5 reshape.445
  163.2 1.0 slice_bitcast_fusion
  164.2 1.0 fusion.41
  168.0 401.2 %while.23 = (s32[]{:T(128)}, f32[6,16,5136]{2,1,0:T(8,128)}, bf16[1280,6,2,16]{0,3,2,1:T(8,128)(2,1)}, s32[1280]{0:T(1024)S(1)}, s32[]{:T(128)}, /*index=5*/f32[...) while((s32[]{:T(128)}, f32[6,16,5136]{2,1,0:T(8,128)}, ...), condition=%wide.region_1.2_spmd.clone, body=%wide.region_0.1_spmd.clone.sunk | while | flops 663332032 | bytes 17449060 | solution.py:97
  169.4 92.5 %fusion.68 = (bf16[1,320,5136]{2,1,0:T(8,128)(2,1)}, bf16[1,320,5136]{2,1,0:T(8,128)(2,1)}) fusion(s32[]{:T(128)} %get-tuple-element.344, s32[320]{0:T(512)S(1)} %get-tuple-element.310, f32[]{:T(128)} %get-tuple-element.343, f32[320]{0:T(512)S(1)} %get-tuple-element.311, pred[]{:T(512)} %get-tuple-element.345, ...), kind=kLoop, calls=%fused_computation.5.clone.1 | loop fusion | flops 27939840 | bytes 6583385 | tf_op jit(solution)/shard_map/convert
  261.9 6.0 %fusion.69 = f32[6,16,5136]{2,1,0:T(8,128)} fusion(bf16[1,320,5136]{2,1,0:T(8,128)(2,1)} %get-tuple-element.312, bf16[1,320,5136]{2,1,0:T(8,128)(2,1)} %get-tuple-element.313, f32[6,16,5136]{2,1,0:T(8,128)} %get-tuple-element.327, pred[]{:T(512)S(6)} %compare.8, bf16[1280,6,2,16]{0,3,2,1:T(8,128)(2,1)} %get-tuple-element.340, s32[]{:T(128)S(6)} %select_n.147), kind=kOutput, calls=%fused_computation.4.clone.1 | convolution fusion | flops 635384832 | bytes 10852357 | tf_op jit(solution)/shard_map/while/body/eval_jaxpr/while/body/eval_jaxpr/sfrl,rsp->flp/dot_general | solution.py:93
  269.3 92.5 %fusion.68 = (bf16[1,320,5136]{2,1,0:T(8,128)(2,1)}, bf16[1,320,5136]{2,1,0:T(8,128)(2,1)}) fusion(s32[]{:T(128)} %get-tuple-element.344, s32[320]{0:T(512)S(1)} %get-tuple-element.310, f32[]{:T(128)} %get-tuple-element.343, f32[320]{0:T(512)S(1)} %get-tuple-element.311, pred[]{:T(512)} %get-tuple-element.345, ...), kind=kLoop, calls=%fused_computation.5.clone.1 | loop fusion | flops 27939840 | bytes 6583385 | tf_op jit(solution)/shard_map/convert
  361.7 6.5 %fusion.69 = f32[6,16,5136]{2,1,0:T(8,128)} fusion(bf16[1,320,5136]{2,1,0:T(8,128)(2,1)} %get-tuple-element.312, bf16[1,320,5136]{2,1,0:T(8,128)(2,1)} %get-tuple-element.313, f32[6,16,5136]{2,1,0:T(8,128)} %get-tuple-element.327, pred[]{:T(512)S(6)} %compare.8, bf16[1280,6,2,16]{0,3,2,1:T(8,128)(2,1)} %get-tuple-element.340, s32[]{:T(128)S(6)} %select_n.147), kind=kOutput, calls=%fused_computation.4.clone.1 | convolution fusion | flops 635384832 | bytes 10852357 | tf_op jit(solution)/shard_map/while/body/eval_jaxpr/while/body/eval_jaxpr/sfrl,rsp->flp/dot_general | solution.py:93
  369.7 92.5 %fusion.68 = (bf16[1,320,5136]{2,1,0:T(8,128)(2,1)}, bf16[1,320,5136]{2,1,0:T(8,128)(2,1)}) fusion(s32[]{:T(128)} %get-tuple-element.344, s32[320]{0:T(512)S(1)} %get-tuple-element.310, f32[]{:T(128)} %get-tuple-element.343, f32[320]{0:T(512)S(1)} %get-tuple-element.311, pred[]{:T(512)} %get-tuple-element.345, ...), kind=kLoop, calls=%fused_computation.5.clone.1 | loop fusion | flops 27939840 | bytes 6583385 | tf_op jit(solution)/shard_map/convert
  462.2 6.5 %fusion.69 = f32[6,16,5136]{2,1,0:T(8,128)} fusion(bf16[1,320,5136]{2,1,0:T(8,128)(2,1)} %get-tuple-element.312, bf16[1,320,5136]{2,1,0:T(8,128)(2,1)} %get-tuple-element.313, f32[6,16,5136]{2,1,0:T(8,128)} %get-tuple-element.327, pred[]{:T(512)S(6)} %compare.8, bf16[1280,6,2,16]{0,3,2,1:T(8,128)(2,1)} %get-tuple-element.340, s32[]{:T(128)S(6)} %select_n.147), kind=kOutput, calls=%fused_computation.4.clone.1 | convolution fusion | flops 635384832 | bytes 10852357 | tf_op jit(solution)/shard_map/while/body/eval_jaxpr/while/body/eval_jaxpr/sfrl,rsp->flp/dot_general | solution.py:93
  470.1 92.5 %fusion.68 = (bf16[1,320,5136]{2,1,0:T(8,128)(2,1)}, bf16[1,320,5136]{2,1,0:T(8,128)(2,1)}) fusion(s32[]{:T(128)} %get-tuple-element.344, s32[320]{0:T(512)S(1)} %get-tuple-element.310, f32[]{:T(128)} %get-tuple-element.343, f32[320]{0:T(512)S(1)} %get-tuple-element.311, pred[]{:T(512)} %get-tuple-element.345, ...), kind=kLoop, calls=%fused_computation.5.clone.1 | loop fusion | flops 27939840 | bytes 6583385 | tf_op jit(solution)/shard_map/convert
  562.6 6.5 %fusion.69 = f32[6,16,5136]{2,1,0:T(8,128)} fusion(bf16[1,320,5136]{2,1,0:T(8,128)(2,1)} %get-tuple-element.312, bf16[1,320,5136]{2,1,0:T(8,128)(2,1)} %get-tuple-element.313, f32[6,16,5136]{2,1,0:T(8,128)} %get-tuple-element.327, pred[]{:T(512)S(6)} %compare.8, bf16[1280,6,2,16]{0,3,2,1:T(8,128)(2,1)} %get-tuple-element.340, s32[]{:T(128)S(6)} %select_n.147), kind=kOutput, calls=%fused_computation.4.clone.1 | convolution fusion | flops 635384832 | bytes 10852357 | tf_op jit(solution)/shard_map/while/body/eval_jaxpr/while/body/eval_jaxpr/sfrl,rsp->flp/dot_general | solution.py:93
  569.2 2.6 convert_element_type.99
  (50 shorter events, 10.5 us)
Async XLA Ops:
  0.0 118.0 %copy-start = (bf16[80,16,1280]{2,1,0:T(8,128)(2,1)S(1)}, bf16[80,16,1280]{2,1,0:T(8,128)(2,1)}, u32[]{:S(2)}) copy-start(bf16[80,16,1280]{2,1,0:T(8,128)(2,1)} %param.10) | copy-start | bytes 9830404
  1.0 16.2 %copy-start.2 = (f32[80,1280]{1,0:T(8,128)}, f32[80,1280]{1,0:T(8,128)S(1)}, u32[]{:S(2)}) copy-start(f32[80,1280]{1,0:T(8,128)S(1)} %fusion.40) | copy-start | bytes 1228804
  81.3 15.9 %slice-start = ((s8[13107200]{0:T(1024)(128)(4,1)}), s8[4194304]{0:T(1024)(128)(4,1)S(1)}, s32[]{:S(2)}) async-start(s8[13107200]{0:T(1024)(128)(4,1)} %bitcast.47), calls=%async_computation.1 | async-start | bytes 8388608
  81.3 17.2 %slice-start.1 = ((s8[13107200]{0:T(1024)(128)(4,1)}), s8[4194304]{0:T(1024)(128)(4,1)S(1)}, s32[]{:S(2)}) async-start(s8[13107200]{0:T(1024)(128)(4,1)} %bitcast.47), calls=%async_computation.2 | async-start | bytes 8388608
  81.3 17.1 %copy-start.1 = (f32[80,32,1280]{2,1,0:T(8,128)S(1)}, f32[80,32,1280]{2,1,0:T(8,128)}, u32[]{:S(2)}) copy-start(f32[80,32,1280]{2,1,0:T(8,128)} %get-tuple-element.225) | copy-start | bytes 39321604
  88.5 11.2 %slice-start.2 = ((s8[13107200]{0:T(1024)(128)(4,1)}), s8[4194304]{0:T(1024)(128)(4,1)S(1)}, s32[]{:S(2)}) async-start(s8[13107200]{0:T(1024)(128)(4,1)} %bitcast.47), calls=%async_computation.3 | async-start | bytes 8388608
  88.5 11.2 %slice-start.3 = ((s8[13107200]{0:T(1024)(128)(4,1)}), s8[524288]{0:T(1024)(128)(4,1)S(1)}, s32[]{:S(2)}) async-start(s8[13107200]{0:T(1024)(128)(4,1)} %bitcast.47), calls=%async_computation.4 | async-start | bytes 1048576
  99.7 4.3 slice-start.4
  101.8 3.5 slice-start.5
  101.8 3.5 copy-start.3
  118.0 24.9 %copy-start.5 = (s32[1280]{0:T(1024)S(1)}, s32[1280]{0:T(1024)}, u32[]{:S(2)}) copy-start(s32[1280]{0:T(1024)} %param.11) | copy-start | bytes 15364
  134.1 24.1 %all-to-all-start = ((f32[16,80,128]{2,1,0:T(8,128)}), f32[16,80,128]{2,1,0:T(8,128)}, u32[]{:S(2)}, u32[]{:S(2)}) async-start(f32[16,80,128]{2,1,0:T(8,128)} %copy.8), calls=%async_computation | async-start | bytes 1310720 | tf_op jit(solution)/shard_map/all_to_all | solution.py:109
  167.2 0.8 copy-start.4
where the time goes:
time: 572 us
  other arithmetic  457 us (80%)
  local copies, waits for them, and re-layouts  51.4 us (9%)
  matrix products  39.6 us (7%)
  waiting for transfers between devices  15.3 us (3%)
  starting transfers between devices  7.45 us (1%)
    another operation x4, other arithmetic  370 us
    slice x1, local copies, waits for them, and re-layouts, meridional(): values[..., 1:]  36.5 us
    mul x1, other arithmetic, meridional(): return (upper_coef * shifted_up - lower_coef * shifted_down) * live_mask  27.6 us
    dot_general x4, matrix products, add_segment(): jnp.einsum('sfrl,rsp->flp', segment, basis, preferred_element_type=jnp.fl...  25.6 us
    unnamed x11, other arithmetic  25.1 us
    all_to_all x1, waiting for transfers between devices, body(): lax.all_to_all(fourier, 'wave', split_axis=0, concat_axis=1, tiled=True)  15.3 us
    dot_general x1, matrix products, body(): jnp.einsum('sck,slk->lsc', spec, legendre, preferred_element_type=jnp.flo...  14 us
    mul x1, other arithmetic, spectral_fields(): potential = delta * inverse[:, None, :]  13.8 us
  transfers between devices with their start and end apart: 1, of which 1 were waited for; matrix products, arithmetic and copies ran while one was open for 0% of the time, Pallas kernels for 0%

commit v1 on v0

v1 whole, which is shorter than its diff:
```python
import functools

import jax
import jax.numpy as jnp
from jax import lax
from jax.experimental import pallas as pl
from jax.experimental.pallas import tpu as pltpu
from jax.sharding import PartitionSpec as P

NLON = 5136
LANES = 128
COS = (1.0, -1 / 2, 1 / 24, -1 / 720, 1 / 40320, -1 / 3628800, 1 / 479001600,
       -1 / 87178291200, 1 / 20922789888000, -1 / 6402373705728000)
SIN = (1.0, -1 / 6, 1 / 120, -1 / 5040, 1 / 362880, -1 / 39916800, 1 / 6227020800,
       -1 / 1307674368000, 1 / 355687428096000, -1 / 121645100408832000)


def slot_block(slots):
    return max(b for b in range(1, 9) if slots % b == 0)


def degree_coefs(wave, count):
    degree = wave + lax.broadcasted_iota(jnp.int32, (wave.shape[0], count), 1)
    living = degree < count
    positive = living & (degree > 0)
    m = wave.astype(jnp.float32)
    n = degree.astype(jnp.float32)
    inverse = jnp.where(positive, -(count / 4.0) / jnp.maximum(n * (n + 1.0), 1.0), 0.0)

    def eps(x):
        return jnp.sqrt(jnp.maximum(x * x - m * m, 0.0) / jnp.maximum(4.0 * x * x - 1.0, 1.0))

    lower = jnp.where(positive, eps(n), 0.0)
    upper = jnp.where(degree + 1 < count, eps(n + 1.0), 0.0)
    live = living.astype(jnp.float32)
    return live, inverse * m, inverse * (n + 1.0) * lower, -inverse * n * upper


def slot_fourier(values, live, along, before, after, zd):
    count = values.shape[-1]
    p = values.astype(jnp.float32)
    lon = p * along
    lat = pltpu.roll(p, 1, 1) * before + pltpu.roll(p, count - 1, 1) * after
    left = jnp.concatenate([p * live, lon, lat], axis=0).astype(jnp.bfloat16)
    sums = lax.dot_general(left, zd, (((1,), (1,)), ((), ())), preferred_element_type=jnp.float32)
    rows = p.shape[0]
    lev = zd.shape[0] // 4
    plain, a, b = sums[:rows], sums[rows : 2 * rows], sums[2 * rows :]
    zr, zi, dr, di = (slice(g * lev, (g + 1) * lev) for g in range(4))
    turned = jnp.concatenate([-a[:, di], a[:, dr], -a[:, zi], a[:, zr]], axis=1)
    lane = lax.broadcasted_iota(jnp.int32, b.shape, 1)
    winds = turned + jnp.where(lane < 2 * lev, -b, b)
    return jnp.concatenate([winds, plain], axis=1)


def legendre_kernel(wave_ref, zeta_ref, delta_ref, values_ref, out_ref):
    count = zeta_ref.shape[-1]
    coefs = degree_coefs(wave_ref[0], count)
    for s in range(zeta_ref.shape[0]):
        zd = jnp.concatenate([zeta_ref[s], delta_ref[s]], axis=0)
        out = slot_fourier(values_ref[s], *(c[s : s + 1] for c in coefs), zd)
        out_ref[s] = out.astype(out_ref.dtype)


def legendre_sums(waves, vorticity, divergence, legendre):
    slots, columns, count = vorticity.shape
    cycles = legendre.shape[1]
    sb = slot_block(slots)
    block = lambda rows: pl.BlockSpec((sb, rows, count), lambda i: (i, 0, 0))
    return pl.pallas_call(
        legendre_kernel,
        grid=(slots // sb,),
        in_specs=[
            pl.BlockSpec((1, sb, 1), lambda i: (i, 0, 0)),
            block(columns),
            block(columns),
            block(cycles),
        ],
        out_specs=pl.BlockSpec((sb, cycles, 4 * columns), lambda i: (i, 0, 0)),
        out_shape=jax.ShapeDtypeStruct((slots, cycles, 4 * columns), jnp.bfloat16),
    )(waves.reshape(slots // sb, sb, 1), vorticity, divergence, legendre)


def horner(coefs, x):
    total = jnp.full_like(x, coefs[-1])
    for c in coefs[-2::-1]:
        total = total * x + c
    return total


def turn(steps, points, per_point):
    turns = jnp.round(steps * per_point)
    theta = (steps - turns * points) * (per_point * (2.0 * jnp.pi))
    square = theta * theta
    return horner(COS, square), theta * horner(SIN, square)


def fill_basis(row, points, basis):
    slots = row.shape[1]
    tiles = basis.shape[1] // LANES
    per_point = 1.0 / points
    column = lambda x: jnp.broadcast_to(x, (LANES, slots)).T
    wave = column(row)
    step_c, step_s = (column(x) for x in turn(row * float(LANES), points, per_point))
    lane = lax.broadcasted_iota(jnp.int32, (16, LANES), 1).astype(jnp.float32)
    for start in range(0, slots, 16):
        rows = slice(start, start + 16)
        c, s = turn(wave[rows] * lane, points, per_point)
        cs, ss = step_c[rows], step_s[rows]
        for t in range(tiles):
            at = slice(t * LANES, (t + 1) * LANES)
            basis[rows, at] = c.astype(basis.dtype)
            basis[slots + start : slots + start + 16, at] = s.astype(basis.dtype)
            c, s = c * cs - s * ss, s * cs + c * ss


def fill_fields(arrived, wave, points, cosine_sq, count, packed):
    x = arrived.astype(jnp.float32).T
    lev = x.shape[0] // 8
    ur, ui, vr, vi, zr, zi, dr, di = (x[g * lev : (g + 1) * lev] for g in range(8))
    slots = wave.shape[1]
    m = wave.astype(jnp.float32)
    q = m * (4.0 / count)
    over = 1.0 / jnp.full_like(m, cosine_sq)
    ulr, uli, vlr, vli = -q * ui, q * ur, -q * vi, q * vr
    fields = (
        (ur, ui), (vr, vi), (ulr, uli), (vlr, vli),
        (vlr * over - zr, vli * over - zi), (dr - ulr * over, di - uli * over),
    )
    weight = jnp.where(2 * wave < points, jnp.where(wave == 0, 1.0, 2.0), 0.0)
    for f, (re, im) in enumerate(fields):
        a, b = re * weight, -im * weight
        for j in range(4):
            phase = (wave * j) & 3
            c = jnp.where(phase == 0, 1.0, jnp.where(phase == 2, -1.0, 0.0))
            s = jnp.where(phase == 1, 1.0, jnp.where(phase == 3, -1.0, 0.0))
            start = (j * len(fields) + f) * lev
            rows = slice(start, start + lev)
            packed[rows, :slots] = (a * c + b * s).astype(packed.dtype)
            packed[rows, slots:] = (b * c - a * s).astype(packed.dtype)


def place(quarters, points, line):
    rows = quarters.shape[0] // 4
    tiles = quarters.shape[1] // LANES
    quarter = points // 4
    lane = lax.broadcasted_iota(jnp.int32, (rows, LANES), 1)
    line[...] = jnp.zeros_like(line)
    for j in range(4):
        offset = quarter * j
        base = pl.multiple_of(offset // LANES * LANES, LANES)
        shift = offset - base
        previous = jnp.zeros((rows, LANES), jnp.float32)
        for t in range(tiles + 1):
            rolled = jnp.zeros((rows, LANES), jnp.float32)
            if t < tiles:
                tile = quarters[j * rows : (j + 1) * rows, t * LANES : (t + 1) * LANES]
                tile = jnp.where(lane + t * LANES < quarter, tile.astype(jnp.float32), 0.0)
                rolled = pltpu.roll(tile, shift, 1)
            moved = jnp.where(lane < shift, previous, rolled).astype(line.dtype)
            at = pl.ds(pl.multiple_of(base + t * LANES, LANES), LANES)
            line[:, at] = line[:, at] + moved
            previous = rolled


def synthesis_kernel(count, points_ref, cosine_ref, wave_ref, arrived_ref, out_ref, basis, packed, quarters, line):
    cycle = pl.program_id(0)
    points = points_ref[cycle]
    wave = wave_ref[...]
    points_f = jnp.full(wave.shape, points, jnp.int32).astype(jnp.float32)
    fill_basis(wave.astype(jnp.float32), points_f[:1, :1], basis)
    fill_fields(arrived_ref[0], wave, points, cosine_ref[cycle], count, packed)
    width = quarters.shape[1]
    for start in range(0, width, 256):
        at = slice(start, min(start + 256, width))
        quarters[:, at] = jnp.dot(
            packed[...], basis[:, at], preferred_element_type=jnp.float32
        ).astype(quarters.dtype)
    place(quarters, points, line)
    out_ref[0] = line[:, : out_ref.shape[2]]


def synthesis(arrived, waves, points, cosine_sq, count):
    cycles, slots, columns = arrived.shape
    rows = 6 * columns // 8
    width = -(-NLON // 4 // LANES) * LANES
    return pl.pallas_call(
        functools.partial(synthesis_kernel, count),
        grid=(cycles,),
        in_specs=[
            pl.BlockSpec(memory_space=pltpu.SMEM),
            pl.BlockSpec(memory_space=pltpu.SMEM),
            pl.BlockSpec((1, slots), lambda i: (0, 0)),
            pl.BlockSpec((1, slots, columns), lambda i: (i, 0, 0)),
        ],
        out_specs=pl.BlockSpec((1, rows, NLON), lambda i: (i, 0, 0)),
        out_shape=jax.ShapeDtypeStruct((cycles, rows, NLON), jnp.bfloat16),
        scratch_shapes=[
            pltpu.VMEM((2 * slots, width), jnp.bfloat16),
            pltpu.VMEM((4 * rows, 2 * slots), jnp.bfloat16),
            pltpu.VMEM((4 * rows, width), jnp.bfloat16),
            pltpu.VMEM((rows, 4 * width + 2 * LANES), jnp.bfloat16),
        ],
    )(points, cosine_sq, waves.reshape(1, slots), arrived)


def body(vorticity, divergence, legendre, wave_of_slot, cycle_points, cos_squared):
    slots, _, count = vorticity.shape
    offset = lax.axis_index("wave") * slots
    own = lax.dynamic_slice_in_dim(wave_of_slot, offset, slots, 0)
    fourier = legendre_sums(own, vorticity, divergence, legendre)
    fourier = jnp.swapaxes(fourier, 0, 1)
    arrived = lax.all_to_all(fourier, "wave", split_axis=0, concat_axis=1, tiled=True)
    return synthesis(arrived, wave_of_slot, cycle_points, cos_squared, count)


def solution(mesh):
    return jax.shard_map(
        body,
        mesh=mesh,
        in_specs=(
            P(("member", "wave"), None, None),
            P(("member", "wave"), None, None),
            P("wave", None, None),
            P(),
            P("wave"),
            P("wave"),
        ),
        out_specs=P(("member", "wave"), None, None),
        check_vma=False,
    )
```

time: 572 us -> 43.5 us (0.08)
  other arithmetic: 457 us -> 0 us
  local copies, waits for them, and re-layouts: 51.4 us -> 4.62 us
  matrix products: 39.6 us -> 0 us
  Pallas kernels: 0 us -> 20.4 us
  waiting for transfers between devices: 15.3 us -> 9.17 us
    another operation x6 -> x0, other arithmetic: 371 us -> none
    mul x3 -> x0, other arithmetic: 42.4 us -> none  [the longest x1 27.6 us: meridional(): return (upper_coef * shifted_up - lower_coef * shifted_down) * live_mask]
    dot_general x5 -> x0, matrix products: 39.6 us -> none  [the longest x4 25.6 us: add_segment(): jnp.einsum('sfrl,rsp->flp', segment, basis, preferred_element_type=jnp.fl...]
    slice x2 -> x0, local copies, waits for them, and re-layouts: 36.7 us -> none  [the longest x1 36.5 us: meridional(): values[..., 1:]]
    unnamed x11 -> x0, other arithmetic: 25.1 us -> none
    pallas_call x0 -> x2, Pallas kernels: none -> 20.4 us  [the longest x1 12.5 us: legendre_sums(): pl.pallas_call(legendre_kernel, grid=(slots // sb,), in_specs=[pl.BlockSp...]
    concatenate x1 -> x0, other arithmetic: 7.8 us -> none  [spectral_fields(): jnp.concatenate([u_real, u_imag, v_real, v_imag, zeta, delta], axis=1)]
    all_to_all x1, waiting for transfers between devices: 15.3 us -> 9.17 us  [body(): lax.all_to_all(fourier, 'wave', split_axis=0, concat_axis=1, tiled=True)]
  transfers between devices with their start and end apart: 1 -> 1, of which waited for: 1 -> 1; matrix products, arithmetic and copies ran while one was open for 0% -> 1% of each run, Pallas kernels for 0% -> 0%
where the time goes in v1:
time: 43.5 us; the launch traced here: 42.9 us
  Pallas kernels  20.4 us (47%)
  waiting for transfers between devices  9.17 us (21%)
  starting transfers between devices  7.4 us (17%)
  local copies, waits for them, and re-layouts  4.62 us (11%)
  between operations  1.32 us (3%)
    pallas_call x1, Pallas kernels, legendre_sums(): pl.pallas_call(legendre_kernel, grid=(slots // sb,), in_specs=[pl.BlockSp...  12.5 us
    all_to_all x1, waiting for transfers between devices, body(): lax.all_to_all(fourier, 'wave', split_axis=0, concat_axis=1, tiled=True)  9.17 us
    pallas_call x1, Pallas kernels, synthesis(): pl.pallas_call(functools.partial(synthesis_kernel, count), grid=(cycles,)...  7.93 us
    all_to_all x1, starting transfers between devices, body(): lax.all_to_all(fourier, 'wave', split_axis=0, concat_axis=1, tiled=True)  7.4 us
    transpose x1, local copies, waits for them, and re-layouts, body(): fourier = jnp.swapaxes(fourier, 0, 1)  1.77 us
  transfers between devices with their start and end apart: 1, of which 1 were waited for; matrix products, arithmetic and copies ran while one was open for 1% of the time, Pallas kernels for 0%

profile of v1, /device:TPU:0, one launch (start us, length us, event | category | flops | bytes accessed | tf_op | source)
XLA Modules:
  0.0 42.9 jit_solution(2136814282856174919)
XLA Ops:
  0.0 0.8 %dynamic_slice.3 = s32[80]{0:T(128)S(1)} dynamic-slice(s32[1280]{0:T(1024)} %param.9, s32[]{:T(128)S(6)} %select_n.3), dynamic_slice_sizes={80} | dynamic-slice | bytes 644 | tf_op jit(solution)/shard_map/dynamic_slice | solution.py:210
  0.8 0.8 %reshape.11.wave_ref = s32[10,8,1]{2,1,0:T(8,128)} reshape(s32[80]{0:T(128)S(1)} %dynamic_slice.3) | data formatting | bytes 640 | tf_op jit(solution)/shard_map/reshape | solution.py:81
  1.5 0.0 copy-start.1
  1.5 12.5 %shard_map.64 = bf16[80,16,128]{2,1,0:T(8,128)(2,1)} custom-call(s32[10,8,1]{2,1,0:T(8,128)} %reshape.11.wave_ref, bf16[80,32,1280]{2,1,0:T(8,128)(2,1)} %zeta_ref.1, bf16[80,32,1280]{2,1,0:T(8,128)(2,1)} %delta_ref.1, bf16[80,16,1280]{2,1,0:T(8,128)(2,1)} %values_ref.1), custom_call_target="tpu_custom_call" | custom-call | tf_op jit(solution)/shard_map/pallas_call | solution.py:70
  14.0 1.8 %copy.12 = bf16[16,80,128]{2,1,0:T(8,128)(2,1)} copy(bf16[16,80,128]{2,0,1:T(8,128)(2,1)} %bitcast.3) | data formatting | bytes 655360 | tf_op jit(solution)/shard_map/transpose | solution.py:212
  15.8 7.4 %all-to-all-start = ((bf16[16,80,128]{2,1,0:T(8,128)(2,1)}), bf16[16,80,128]{2,1,0:T(8,128)(2,1)S(1)}, u32[]{:S(2)}, u32[]{:S(2)}) async-start(bf16[16,80,128]{2,1,0:T(8,128)(2,1)} %copy.12), calls=%async_computation | async-start | bytes 655360 | tf_op jit(solution)/shard_map/all_to_all | solution.py:213
  23.2 0.0 copy-done.1
  23.2 0.6 %reshape.9.wave_ref = s32[1,1280]{1,0:T(1,128)} reshape(s32[1280]{0:T(1024)S(1)} %copy-done.1) | data formatting | bytes 10240 | tf_op jit(solution)/shard_map/reshape | solution.py:204
  25.1 9.2 %all-to-all-done = bf16[16,80,128]{2,1,0:T(8,128)(2,1)S(1)} async-done(((bf16[16,80,128]{2,1,0:T(8,128)(2,1)}), bf16[16,80,128]{2,1,0:T(8,128)(2,1)S(1)}, u32[]{:S(2)}, u32[]{:S(2)}) %all-to-all-start) | async-done | bytes 327712 | tf_op jit(solution)/shard_map/all_to_all | solution.py:213
  34.3 0.0 copy-start
  34.3 0.7 %copy-done = bf16[16,80,128]{2,1,0:T(8,128)(2,1)} copy-done((bf16[16,80,128]{2,1,0:T(8,128)(2,1)}, bf16[16,80,128]{2,1,0:T(8,128)(2,1)S(1)}, u32[]{:S(2)}) %copy-start) | copy-done | bytes 327704
  35.0 7.9 %shard_map.65 = bf16[1,96,5136]{2,1,0:T(8,128)(2,1)} custom-call(s32[1]{0:T(128)S(6)} %copy.13.points_ref, f32[1]{0:T(128)S(6)} %copy.14.cosine_ref, s32[1,1280]{1,0:T(1,128)} %reshape.9.wave_ref, bf16[1,1280,128]{2,1,0:T(8,128)(2,1)} %bitcast.2), custom_call_target="tpu_custom_call" | custom-call | tf_op jit(solution)/shard_map/pallas_call | solution.py:187
Async XLA Ops:
  1.5 21.7 %copy-start.1 = (s32[1280]{0:T(1024)S(1)}, s32[1280]{0:T(1024)}, u32[]{:S(2)}) copy-start(s32[1280]{0:T(1024)} %param.9) | copy-start | bytes 15364
  15.8 18.5 %all-to-all-start = ((bf16[16,80,128]{2,1,0:T(8,128)(2,1)}), bf16[16,80,128]{2,1,0:T(8,128)(2,1)S(1)}, u32[]{:S(2)}, u32[]{:S(2)}) async-start(bf16[16,80,128]{2,1,0:T(8,128)(2,1)} %copy.12), calls=%async_computation | async-start | bytes 655360 | tf_op jit(solution)/shard_map/all_to_all | solution.py:213
  34.3 0.7 %copy-start = (bf16[16,80,128]{2,1,0:T(8,128)(2,1)}, bf16[16,80,128]{2,1,0:T(8,128)(2,1)S(1)}, u32[]{:S(2)}) copy-start(bf16[16,80,128]{2,1,0:T(8,128)(2,1)S(1)} %all-to-all-done) | copy-start | bytes 983044

commit v2 on v1

--- a/solution.py
+++ b/solution.py
@@ -16,7 +16,7 @@
 
 
 def slot_block(slots):
-    return max(b for b in range(1, 9) if slots % b == 0)
+    return max(b for b in range(1, 17) if slots % b == 0)
 
 
 def degree_coefs(wave, count):
@@ -53,34 +53,6 @@
     return jnp.concatenate([winds, plain], axis=1)
 
 
-def legendre_kernel(wave_ref, zeta_ref, delta_ref, values_ref, out_ref):
-    count = zeta_ref.shape[-1]
-    coefs = degree_coefs(wave_ref[0], count)
-    for s in range(zeta_ref.shape[0]):
-        zd = jnp.concatenate([zeta_ref[s], delta_ref[s]], axis=0)
-        out = slot_fourier(values_ref[s], *(c[s : s + 1] for c in coefs), zd)
-        out_ref[s] = out.astype(out_ref.dtype)
-
-
-def legendre_sums(waves, vorticity, divergence, legendre):
-    slots, columns, count = vorticity.shape
-    cycles = legendre.shape[1]
-    sb = slot_block(slots)
-    block = lambda rows: pl.BlockSpec((sb, rows, count), lambda i: (i, 0, 0))
-    return pl.pallas_call(
-        legendre_kernel,
-        grid=(slots // sb,),
-        in_specs=[
-            pl.BlockSpec((1, sb, 1), lambda i: (i, 0, 0)),
-            block(columns),
-            block(columns),
-            block(cycles),
-        ],
-        out_specs=pl.BlockSpec((sb, cycles, 4 * columns), lambda i: (i, 0, 0)),
-        out_shape=jax.ShapeDtypeStruct((slots, cycles, 4 * columns), jnp.bfloat16),
-    )(waves.reshape(slots // sb, sb, 1), vorticity, divergence, legendre)
-
-
 def horner(coefs, x):
     total = jnp.full_like(x, coefs[-1])
     for c in coefs[-2::-1]:
@@ -95,19 +67,22 @@
     return horner(COS, square), theta * horner(SIN, square)
 
 
-def fill_basis(row, points, basis):
+def basis_columns(row, points):
     slots = row.shape[1]
-    tiles = basis.shape[1] // LANES
-    per_point = 1.0 / points
     column = lambda x: jnp.broadcast_to(x, (LANES, slots)).T
-    wave = column(row)
-    step_c, step_s = (column(x) for x in turn(row * float(LANES), points, per_point))
+    step = turn(row * float(LANES), points, 1.0 / points)
+    return column(row), column(step[0]), column(step[1])
+
+
+def fill_basis(columns, points, basis, first, last):
+    wave, step_c, step_s = columns
+    slots = wave.shape[0]
     lane = lax.broadcasted_iota(jnp.int32, (16, LANES), 1).astype(jnp.float32)
-    for start in range(0, slots, 16):
+    for start in range(first, last, 16):
         rows = slice(start, start + 16)
-        c, s = turn(wave[rows] * lane, points, per_point)
+        c, s = turn(wave[rows] * lane, points, 1.0 / points)
         cs, ss = step_c[rows], step_s[rows]
-        for t in range(tiles):
+        for t in range(basis.shape[1] // LANES):
             at = slice(t * LANES, (t + 1) * LANES)
             basis[rows, at] = c.astype(basis.dtype)
             basis[slots + start : slots + start + 16, at] = s.astype(basis.dtype)
@@ -163,55 +138,159 @@
             previous = rolled
 
 
-def synthesis_kernel(count, points_ref, cosine_ref, wave_ref, arrived_ref, out_ref, basis, packed, quarters, line):
-    cycle = pl.program_id(0)
-    points = points_ref[cycle]
-    wave = wave_ref[...]
-    points_f = jnp.full(wave.shape, points, jnp.int32).astype(jnp.float32)
-    fill_basis(wave.astype(jnp.float32), points_f[:1, :1], basis)
-    fill_fields(arrived_ref[0], wave, points, cosine_ref[cycle], count, packed)
-    width = quarters.shape[1]
-    for start in range(0, width, 256):
-        at = slice(start, min(start + 256, width))
-        quarters[:, at] = jnp.dot(
-            packed[...], basis[:, at], preferred_element_type=jnp.float32
-        ).astype(quarters.dtype)
-    place(quarters, points, line)
+def exchange_kernel(
+    points_ref, cosine_ref, slots_ref, wave_ref, zeta_ref, delta_ref, values_ref, quarters_ref,
+    sums, sent, held, basis, packed, send_sem, recv_sem,
+):
+    step = pl.program_id(0)
+    cycles, devices, blocks, sb, columns = held.shape
+    count = zeta_ref.shape[-1]
+    me = lax.axis_index("wave")
+    barrier = pltpu.get_barrier_semaphore()
+
+    def copy(block, off, cycle):
+        to = lax.rem(me + off, devices)
+        return pltpu.make_async_remote_copy(
+            src_ref=sent.at[block, to * cycles + cycle],
+            dst_ref=held.at[cycle, me, block],
+            send_sem=send_sem.at[block, cycle, off - 1],
+            recv_sem=recv_sem.at[block, cycle, off - 1],
+            device_id={"wave": to},
+            device_id_type=pl.DeviceIdType.MESH,
+        )
+
+    def send(block):
+        for cycle in range(cycles):
+            pl.loop(1, devices)(lambda off: copy(block, off, cycle).start())
+
+    @pl.when(step == 0)
+    def _():
+        @pl.loop(1, devices)
+        def _(off):
+            pl.semaphore_signal(
+                barrier, inc=1, device_id={"wave": lax.rem(me + off, devices)},
+                device_id_type=pl.DeviceIdType.MESH,
+            )
+
+    @pl.when(step == 1)
+    def _():
+        pl.semaphore_wait(barrier, devices - 1)
+
+    @pl.when(step > 0)
+    def _():
+        send(step - 1)
+
+    first = me * (blocks * sb) + step * sb
+    row = lax.broadcasted_iota(jnp.int32, (sb, 1), 0)
+    waves = jnp.zeros((sb, 1), jnp.int32)
+    for s in range(sb):
+        waves = jnp.where(row == s, slots_ref[first + s], waves)
+    coefs = degree_coefs(waves, count)
+    rows = values_ref.shape[1]
+    for s in range(sb):
+        zd = jnp.concatenate([zeta_ref[s], delta_ref[s]], axis=0)
+        out = slot_fourier(values_ref[s], *(c[s : s + 1] for c in coefs), zd)
+        sums[pl.ds(s, rows, sb), :] = out
+    sent[step] = sums[...].astype(sent.dtype).reshape(rows, sb, columns)
+
+    @pl.when(step == blocks - 1)
+    def _():
+        wave = wave_ref[...].reshape(1, -1)
+        slots = wave.shape[1]
+        for cycle in range(cycles):
+            points = points_ref[cycle]
+            points_f = jnp.full((1, 1), points, jnp.int32).astype(jnp.float32)
+            cols = basis_columns(wave.astype(jnp.float32), points_f)
+            early = slots // 4 // 16 * 16
+            fill_basis(cols, points_f, basis, 0, early)
+            if cycle == 0:
+                send(blocks - 1)
+            fill_basis(cols, points_f, basis, early, slots)
+            if cycle == 0:
+                for c in range(cycles):
+                    for block in range(blocks):
+                        held[c, me, block] = sent[block, me * cycles + c]
+
+                        @pl.loop(1, devices)
+                        def _(off):
+                            copy(block, off, c).wait_recv()
+            arrived = held[cycle].reshape(slots, columns)
+            fill_fields(arrived, wave, points, cosine_ref[cycle], count, packed)
+            width = basis.shape[1]
+            for start in range(0, width, 256):
+                at = slice(start, min(start + 256, width))
+                quarters_ref[cycle, :, at] = jnp.dot(
+                    packed[...], basis[:, at], preferred_element_type=jnp.float32
+                ).astype(quarters_ref.dtype)
+        for c in range(cycles):
+            for block in range(blocks):
+
+                @pl.loop(1, devices)
+                def _(off):
+                    copy(block, off, c).wait_send()
+
+
+def cycle_quarters(points, cosine_sq, wave_of_slot, vorticity, divergence, legendre):
+    slots, half, count = vorticity.shape
+    lines = legendre.shape[1]
+    cycles = points.shape[0]
+    devices = lines // cycles
+    columns = 4 * half
+    rows = 6 * half
+    width = -(-NLON // 4 // LANES) * LANES
+    sb = slot_block(slots)
+    blocks = slots // sb
+    block = lambda n: pl.BlockSpec((sb, n, count), lambda i: (i, 0, 0))
+    smem = pl.BlockSpec(memory_space=pltpu.SMEM)
+    sem = pltpu.SemaphoreType.DMA((blocks, cycles, devices - 1))
+    return pl.pallas_call(
+        exchange_kernel,
+        grid=(blocks,),
+        in_specs=[
+            smem, smem, smem, pl.BlockSpec(memory_space=pltpu.VMEM),
+            block(half), block(half), block(lines),
+        ],
+        out_specs=pl.BlockSpec((cycles, 2 * rows, width), lambda i: (0, 0, 0)),
+        out_shape=jax.ShapeDtypeStruct((cycles, 2 * rows, width), jnp.bfloat16),
+        scratch_shapes=[
+            pltpu.VMEM((lines * sb, columns), jnp.float32),
+            pltpu.VMEM((blocks, lines, sb, columns), jnp.bfloat16),
+            pltpu.VMEM((cycles, devices, blocks, sb, columns), jnp.bfloat16),
+            pltpu.VMEM((2 * devices * slots, width), jnp.bfloat16),
+            pltpu.VMEM((2 * rows, 2 * devices * slots), jnp.bfloat16),
+            sem,
+            sem,
+        ],
+        compiler_params=pltpu.CompilerParams(collective_id=0, has_side_effects=True),
+    )(points, cosine_sq, wave_of_slot, wave_of_slot, vorticity, divergence, legendre)
+
+
+def place_kernel(points_ref, quarters_ref, out_ref, line):
+    place(quarters_ref.at[0], points_ref[pl.program_id(0)], line)
     out_ref[0] = line[:, : out_ref.shape[2]]
 
 
-def synthesis(arrived, waves, points, cosine_sq, count):
-    cycles, slots, columns = arrived.shape
-    rows = 6 * columns // 8
-    width = -(-NLON // 4 // LANES) * LANES
+def placed(quarters, points):
+    cycles, rows, width = quarters.shape
+    rows = rows // 4
     return pl.pallas_call(
-        functools.partial(synthesis_kernel, count),
+        place_kernel,
         grid=(cycles,),
         in_specs=[
             pl.BlockSpec(memory_space=pltpu.SMEM),
-            pl.BlockSpec(memory_space=pltpu.SMEM),
-            pl.BlockSpec((1, slots), lambda i: (0, 0)),
-            pl.BlockSpec((1, slots, columns), lambda i: (i, 0, 0)),
+            pl.BlockSpec((1, 4 * rows, width), lambda i: (i, 0, 0)),
         ],
         out_specs=pl.BlockSpec((1, rows, NLON), lambda i: (i, 0, 0)),
         out_shape=jax.ShapeDtypeStruct((cycles, rows, NLON), jnp.bfloat16),
-        scratch_shapes=[
-            pltpu.VMEM((2 * slots, width), jnp.bfloat16),
-            pltpu.VMEM((4 * rows, 2 * slots), jnp.bfloat16),
-            pltpu.VMEM((4 * rows, width), jnp.bfloat16),
-            pltpu.VMEM((rows, 4 * width + 2 * LANES), jnp.bfloat16),
-        ],
-    )(points, cosine_sq, waves.reshape(1, slots), arrived)
+        scratch_shapes=[pltpu.VMEM((rows, 4 * width + 2 * LANES), jnp.bfloat16)],
+    )(points, quarters)
 
 
 def body(vorticity, divergence, legendre, wave_of_slot, cycle_points, cos_squared):
-    slots, _, count = vorticity.shape
-    offset = lax.axis_index("wave") * slots
-    own = lax.dynamic_slice_in_dim(wave_of_slot, offset, slots, 0)
-    fourier = legendre_sums(own, vorticity, divergence, legendre)
-    fourier = jnp.swapaxes(fourier, 0, 1)
-    arrived = lax.all_to_all(fourier, "wave", split_axis=0, concat_axis=1, tiled=True)
-    return synthesis(arrived, wave_of_slot, cycle_points, cos_squared, count)
+    quarters = cycle_quarters(
+        cycle_points, cos_squared, wave_of_slot, vorticity, divergence, legendre
+    )
+    return placed(quarters, cycle_points)
 
 
 def solution(mesh):

time: 43.5 us -> 29.8 us (0.69)
  waiting for transfers between devices: 9.17 us -> 0 us
  Pallas kernels: 20.4 us -> 28.3 us
  starting transfers between devices: 7.4 us -> 0 us
  local copies, waits for them, and re-layouts: 4.62 us -> 0 us
    all_to_all x1 -> x0, waiting for transfers between devices: 9.17 us -> none  [body(): lax.all_to_all(fourier, 'wave', split_axis=0, concat_axis=1, tiled=True)]
    pallas_call x2, Pallas kernels: 20.4 us -> 28.3 us  [the longest x1 25.5 us: cycle_quarters(): pl.pallas_call(exchange_kernel, grid=(blocks,), in_specs=[smem, smem, sme...]
    all_to_all x1 -> x0, starting transfers between devices: 7.4 us -> none  [body(): lax.all_to_all(fourier, 'wave', split_axis=0, concat_axis=1, tiled=True)]
    transpose x1 -> x0, local copies, waits for them, and re-layouts: 1.77 us -> none  [body(): fourier = jnp.swapaxes(fourier, 0, 1)]
    reshape x2 -> x0, local copies, waits for them, and re-layouts: 1.36 us -> none  [the longest x1 0.77 us: legendre_sums(): waves.reshape(slots // sb, sb, 1)]
    dynamic_slice x1 -> x0, local copies, waits for them, and re-layouts: 0.77 us -> none  [body(): own = lax.dynamic_slice_in_dim(wave_of_slot, offset, slots, 0)]
    unnamed x4 -> x0, local copies, waits for them, and re-layouts: 0.72 us -> none
  transfers between devices with their start and end apart: 1 -> 0, of which waited for: 1 -> 0; matrix products, arithmetic and copies ran while one was open for 1% -> 0% of each run, Pallas kernels for 0% -> 0%
where the time goes in v2:
time: 29.8 us; the launch traced here: 29.7 us
  Pallas kernels  28.3 us (95%)
  between operations  1.31 us (4%)
    pallas_call x1, Pallas kernels, cycle_quarters(): pl.pallas_call(exchange_kernel, grid=(blocks,), in_specs=[smem, smem, sme...  25.5 us
    pallas_call x1, Pallas kernels, placed(): pl.pallas_call(place_kernel, grid=(cycles,), in_specs=[pl.BlockSpec(memor...  2.81 us

profile of v2, /device:TPU:0, one launch (start us, length us, event | category | flops | bytes accessed | tf_op | source)
XLA Modules:
  0.0 29.7 jit_solution(1750207673287521097)
XLA Ops:
  1.3 25.5 %shard_map.64.quarters_ref = bf16[1,384,1408]{2,1,0:T(8,128)(2,1)} custom-call(s32[1]{0:T(128)S(6)} %copy.7.points_ref, f32[1]{0:T(128)S(6)} %copy.8.cosine_ref, s32[1280]{0:T(1024)} %wave_ref.1, s32[1280]{0:T(1024)} %wave_ref.1, bf16[80,32,1280]{2,1,0:T(8,128)(2,1)} %zeta_ref.1, bf16[80,32,1280]{2,1,0:T(8,128)(2,1)} %delta_ref.1, ...), custom_call_target="tpu_custom_call" | custom-call | tf_op jit(solution)/shard_map/pallas_call | solution.py:246
  26.8 2.8 %shard_map.65 = bf16[1,96,5136]{2,1,0:T(8,128)(2,1)} custom-call(s32[1]{0:T(128)S(6)} %copy.7.points_ref, bf16[1,384,1408]{2,1,0:T(8,128)(2,1)} %shard_map.64.quarters_ref), custom_call_target="tpu_custom_call" | custom-call | tf_op jit(solution)/shard_map/pallas_call | solution.py:276

commit v3 on v2

--- a/solution.py
+++ b/solution.py
@@ -138,8 +138,12 @@
             previous = rolled
 
 
+def send_groups(blocks):
+    return [(0, (blocks + 1) // 2), ((blocks + 1) // 2, blocks)]
+
+
 def exchange_kernel(
-    points_ref, cosine_ref, slots_ref, wave_ref, zeta_ref, delta_ref, values_ref, quarters_ref,
+    groups,     points_ref, cosine_ref, slots_ref, wave_ref, zeta_ref, delta_ref, values_ref, quarters_ref,
     sums, sent, held, basis, packed, send_sem, recv_sem,
 ):
     step = pl.program_id(0)
@@ -148,20 +152,26 @@
     me = lax.axis_index("wave")
     barrier = pltpu.get_barrier_semaphore()
 
-    def copy(block, off, cycle):
+    def copy(group, off, cycle):
+        start, stop = groups[group]
         to = lax.rem(me + off, devices)
         return pltpu.make_async_remote_copy(
-            src_ref=sent.at[block, to * cycles + cycle],
-            dst_ref=held.at[cycle, me, block],
-            send_sem=send_sem.at[block, cycle, off - 1],
-            recv_sem=recv_sem.at[block, cycle, off - 1],
+            src_ref=sent.at[to * cycles + cycle, start:stop],
+            dst_ref=held.at[cycle, me, start:stop],
+            send_sem=send_sem.at[group, cycle, off - 1],
+            recv_sem=recv_sem.at[group, cycle, off - 1],
             device_id={"wave": to},
             device_id_type=pl.DeviceIdType.MESH,
         )
 
-    def send(block):
+    def each(group, act):
         for cycle in range(cycles):
-            pl.loop(1, devices)(lambda off: copy(block, off, cycle).start())
+            pl.loop(1, devices)(lambda off: act(copy(group, off, cycle)))
+
+    def send(group):
+        if group == 0:
+            pl.semaphore_wait(barrier, devices - 1)
+        each(group, lambda c: c.start())
 
     @pl.when(step == 0)
     def _():
@@ -172,13 +182,8 @@
                 device_id_type=pl.DeviceIdType.MESH,
             )
 
-    @pl.when(step == 1)
-    def _():
-        pl.semaphore_wait(barrier, devices - 1)
-
-    @pl.when(step > 0)
-    def _():
-        send(step - 1)
+    for group, (_, stop) in enumerate(groups[:-1]):
+        pl.when(step == stop)(functools.partial(send, group))
 
     first = me * (blocks * sb) + step * sb
     row = lax.broadcasted_iota(jnp.int32, (sb, 1), 0)
@@ -191,7 +196,7 @@
         zd = jnp.concatenate([zeta_ref[s], delta_ref[s]], axis=0)
         out = slot_fourier(values_ref[s], *(c[s : s + 1] for c in coefs), zd)
         sums[pl.ds(s, rows, sb), :] = out
-    sent[step] = sums[...].astype(sent.dtype).reshape(rows, sb, columns)
+    sent[:, step] = sums[...].astype(sent.dtype).reshape(rows, sb, columns)
 
     @pl.when(step == blocks - 1)
     def _():
@@ -204,16 +209,13 @@
             early = slots // 4 // 16 * 16
             fill_basis(cols, points_f, basis, 0, early)
             if cycle == 0:
-                send(blocks - 1)
+                send(len(groups) - 1)
             fill_basis(cols, points_f, basis, early, slots)
             if cycle == 0:
                 for c in range(cycles):
-                    for block in range(blocks):
-                        held[c, me, block] = sent[block, me * cycles + c]
-
-                        @pl.loop(1, devices)
-                        def _(off):
-                            copy(block, off, c).wait_recv()
+                    held[c, me] = sent[me * cycles + c]
+                for group in range(len(groups)):
+                    each(group, lambda c: c.wait_recv())
             arrived = held[cycle].reshape(slots, columns)
             fill_fields(arrived, wave, points, cosine_ref[cycle], count, packed)
             width = basis.shape[1]
@@ -222,12 +224,8 @@
                 quarters_ref[cycle, :, at] = jnp.dot(
                     packed[...], basis[:, at], preferred_element_type=jnp.float32
                 ).astype(quarters_ref.dtype)
-        for c in range(cycles):
-            for block in range(blocks):
-
-                @pl.loop(1, devices)
-                def _(off):
-                    copy(block, off, c).wait_send()
+        for group in range(len(groups)):
+            each(group, lambda c: c.wait_send())
 
 
 def cycle_quarters(points, cosine_sq, wave_of_slot, vorticity, divergence, legendre):
@@ -242,9 +240,10 @@
     blocks = slots // sb
     block = lambda n: pl.BlockSpec((sb, n, count), lambda i: (i, 0, 0))
     smem = pl.BlockSpec(memory_space=pltpu.SMEM)
-    sem = pltpu.SemaphoreType.DMA((blocks, cycles, devices - 1))
+    groups = send_groups(blocks)
+    sem = pltpu.SemaphoreType.DMA((len(groups), cycles, devices - 1))
     return pl.pallas_call(
-        exchange_kernel,
+        functools.partial(exchange_kernel, groups),
         grid=(blocks,),
         in_specs=[
             smem, smem, smem, pl.BlockSpec(memory_space=pltpu.VMEM),
@@ -254,7 +253,7 @@
         out_shape=jax.ShapeDtypeStruct((cycles, 2 * rows, width), jnp.bfloat16),
         scratch_shapes=[
             pltpu.VMEM((lines * sb, columns), jnp.float32),
-            pltpu.VMEM((blocks, lines, sb, columns), jnp.bfloat16),
+            pltpu.VMEM((lines, blocks, sb, columns), jnp.bfloat16),
             pltpu.VMEM((cycles, devices, blocks, sb, columns), jnp.bfloat16),
             pltpu.VMEM((2 * devices * slots, width), jnp.bfloat16),
             pltpu.VMEM((2 * rows, 2 * devices * slots), jnp.bfloat16),

time: 29.8 us -> 28.3 us (0.950)
  Pallas kernels: 28.3 us -> 26.8 us
    pallas_call x1, Pallas kernels: 25.5 us -> 24 us  [cycle_quarters(): pl.pallas_call(functools.partial(exchange_kernel, groups), grid=(blocks,)...]
where the time goes in v3:
time: 28.3 us; the launch traced here: 28.1 us
  Pallas kernels  26.8 us (95%)
  between operations  1.31 us (5%)
    pallas_call x1, Pallas kernels, cycle_quarters(): pl.pallas_call(functools.partial(exchange_kernel, groups), grid=(blocks,)...  24 us
    pallas_call x1, Pallas kernels, placed(): pl.pallas_call(place_kernel, grid=(cycles,), in_specs=[pl.BlockSpec(memor...  2.81 us

profile of v3, /device:TPU:0, one launch (start us, length us, event | category | flops | bytes accessed | tf_op | source)
XLA Modules:
  0.0 28.1 jit_solution(8761987845443450914)
XLA Ops:
  1.3 24.0 %shard_map.64.quarters_ref = bf16[1,384,1408]{2,1,0:T(8,128)(2,1)} custom-call(s32[1]{0:T(128)S(6)} %copy.7.points_ref, f32[1]{0:T(128)S(6)} %copy.8.cosine_ref, s32[1280]{0:T(1024)} %wave_ref.1, s32[1280]{0:T(1024)} %wave_ref.1, bf16[80,32,1280]{2,1,0:T(8,128)(2,1)} %zeta_ref.1, bf16[80,32,1280]{2,1,0:T(8,128)(2,1)} %delta_ref.1, ...), custom_call_target="tpu_custom_call" | custom-call | tf_op jit(solution)/shard_map/pallas_call | solution.py:245
  25.3 2.8 %shard_map.65 = bf16[1,96,5136]{2,1,0:T(8,128)(2,1)} custom-call(s32[1]{0:T(128)S(6)} %copy.7.points_ref, bf16[1,384,1408]{2,1,0:T(8,128)(2,1)} %shard_map.64.quarters_ref), custom_call_target="tpu_custom_call" | custom-call | tf_op jit(solution)/shard_map/pallas_call | solution.py:275
